TPU v7x, 256 devices: a whole 4x4x8 slice. The times are simulated.
256 devices in a mesh: section: 16 (over y, z_hi, core), dp: 16 (over x, z_lo).
Axes of the slice: x: 4, y: 4, z: 8 (z_hi: 2, z_lo: 4; z = z_hi * 4 + z_lo), core: 2. Of those that a mesh axis runs over, the one named last changes fastest.
Arguments:
- student_states: bfloat16 [16, 2048, 2048], P('section', 'dp'), may hold values from -6 to 6
- teacher_states: bfloat16 [64, 2048, 7168], P('section', 'dp'), may hold values from -18 to 18
- projector: bfloat16 [16, 2048, 7168], P('section', None, 'dp'), may hold values from -0.125 to 0.125
- layer_map: int32 [16], replicated, may hold values from 0 to 60, as said below
- boundaries: int32 [17], replicated, may hold values from 0 to 61, as said below
- valid_counts: int32 [16], P('dp'), may hold values from 32 to 128, as said below
Outputs:
- student_grads: bfloat16 [16, 2048, 2048], P('section', 'dp')
- projector_grads: bfloat16 [16, 2048, 7168], P('section', None, 'dp')
- layer_losses: float32 [16], P('section')
Inputs may be any that keep to these rules, and one draw needn't show every extreme that they name: Section k holds 4 or 3 teacher layers, three sections the smaller number; boundaries[0] is 0 and boundaries[16] is 61. Teacher layer layer_map[l] lies on a section from l - 2 to l + 2; student layers 0 and 15 pair with layers of sections 1 and 14, student layers 1 and 14 with layers of sections 3 and 12. `valid_counts`: the valid tokens stand first in their micro-batch; the last micro-batch is full.
All inputs are finite; a program needn't handle non-finite values.
Results may differ from a plain program's by a relative error of at most 0.015.
Values may be sent and summed in bfloat16 or wider, within the bound.
No kernel may reach another device: no remote copies, remote signals or barrier semaphores. Data moves between devices by JAX's collectives and lax.ppermute only.
A program may use at most 128 MiB of HBM per device.

v0:
```python
import jax
import jax.numpy as jnp
from jax import lax
from jax.sharding import Mesh
from jax.sharding import PartitionSpec as P

DP = ("dp_0", "dp_1")
loss_scale = 128.0
norm_eps = 1e-06


def from_behind(block, axis, distance):
    devices = range(lax.axis_size(axis))
    route = [(i - distance, i) for i in devices if i - distance in devices]
    return lax.ppermute(block, axis, route)


def whole_of(x, axes, dim):
    for axis in reversed(axes):
        x = lax.all_gather(x, axis, axis=dim, tiled=True)
    return x


def copy_for_each(x, axis):
    copies = jnp.broadcast_to(x, (lax.axis_size(axis), *x.shape))
    return lax.all_to_all(copies, axis, split_axis=0, concat_axis=0, tiled=True)


def over_copies(x, axis):
    everything = copy_for_each(x, axis)
    return jnp.sum(everything, axis=0)


def lookup(table, index):
    places = jnp.arange(table.shape[0], dtype=jnp.int32)
    return jnp.sum(jnp.where(places == index, table, 0))


def direct_step(piece, offset):
    return from_behind(piece, "section", offset)


def per_device(student_states, teacher_states, projector, layer_map, boundaries, valid_counts):
    sections = lax.axis_size("section")
    here = lax.axis_index("section")
    held_slots = teacher_states.shape[0]
    inner = boundaries[1:sections]
    owners = jnp.sum((inner[None, :] <= layer_map[:, None]).astype(jnp.int32), axis=1)
    first_layer = lookup(boundaries, here)

    def outgoing(offset):
        destination = here + offset
        inside = (destination >= 0) & (destination < sections)
        wanted = lookup(layer_map, destination)
        owner = lookup(owners, destination)
        place = jnp.clip(wanted - first_layer, 0, held_slots - 1)
        piece = lax.dynamic_index_in_dim(teacher_states, place, 0, keepdims=False)
        return jnp.where(inside & (owner == here), piece, jnp.zeros_like(piece))

    needed = here - lookup(owners, here)
    arrivals = []
    for offset in (-2, -1, 1, 2):
        arrivals.append((offset, direct_step(outgoing(offset), offset)))
    hidden = outgoing(0)
    for offset, arrived in arrivals:
        hidden = jnp.where(needed == offset, arrived, hidden)
    wide = hidden.astype(jnp.float32)
    target = (wide * lax.rsqrt(jnp.mean(wide * wide, axis=1, keepdims=True) + norm_eps)).astype(
        jnp.bfloat16
    )
    columns = lax.all_to_all(target, DP, split_axis=1, concat_axis=0, tiled=True)
    students, counts = (whole_of(student_states[0], DP, 0), whole_of(valid_counts, DP, 0))
    per_batch = student_states.shape[1]
    token_rows = jnp.arange(students.shape[0], dtype=jnp.int32)
    batch_index = token_rows // per_batch
    batches = jnp.arange(counts.shape[0], dtype=jnp.int32)
    limit = jnp.sum(jnp.where(batch_index[:, None] == batches[None, :], counts[None, :], 0), axis=1)
    valid = (token_rows % per_batch < limit).astype(jnp.float32)[:, None]
    total = jnp.sum(counts).astype(jnp.float32)
    weights = projector[0]
    projected = jnp.dot(students, weights, preferred_element_type=jnp.float32)
    residual = projected - columns.astype(jnp.float32)
    squares = jnp.sum(valid * residual * residual)
    teacher_width = weights.shape[1] * lax.axis_size(DP)
    loss = over_copies(squares, DP) / (total * teacher_width)
    scaled = (valid * (loss_scale / total) * residual).astype(jnp.bfloat16)
    student_grad = lax.psum_scatter(
        lax.dot_general(
            scaled, weights, (((1,), (1,)), ((), ())), preferred_element_type=jnp.float32
        ).astype(jnp.bfloat16),
        DP,
        scatter_dimension=0,
        tiled=True,
    )
    projector_grad = lax.dot_general(
        students, scaled, (((0,), (0,)), ((), ())), preferred_element_type=jnp.float32
    ).astype(jnp.bfloat16)
    return (student_grad[None], projector_grad[None], jnp.reshape(loss, (1,)))


def solution(mesh):
    split = Mesh(mesh.devices.reshape(mesh.shape["section"], 4, 4), ("section", "dp_0", "dp_1"))
    return jax.shard_map(
        per_device,
        mesh=split,
        in_specs=(
            P("section", DP, None),
            P("section", DP, None),
            P("section", None, DP),
            P(),
            P(),
            P(DP),
        ),
        out_specs=(P("section", DP, None), P("section", None, DP), P("section")),
        check_vma=False,
    )
```

profile of v0, /device:TPU:1, one launch (start us, length us, event | category | flops | bytes accessed | tf_op | source)
XLA Modules:
  0.0 574.9 jit_solution(18182196803726800490)
XLA Ops:
  7.2 0.0 copy-start
  7.2 0.0 all-gather.5.cloned.1.call-start
  7.2 0.7 all-gather.5.cloned.1.call-update
  7.9 0.0 all-gather.7.cloned.1.call-start
  8.0 0.7 slice.3
  8.7 1.4 fusion.36
  10.1 0.8 convert_reduce_fusion
  10.9 1.5 fusion.26
  19.4 7.4 %constant_dynamic-slice_fusion = (bf16[1,128,7168]{2,1,0:T(8,128)(2,1)}, bf16[1,128,7168]{2,1,0:T(8,128)(2,1)}, bf16[1,128,7168]{2,1,0:T(8,128)(2,1)}, bf16[1,128,7168]{2,1,0:T(8,128)(2,1)}, bf16[1,128,7168]{2,1,0:T(8,128)(2,1)}) fusion(bf16[4,128,7168]{2,1,0:T(8,128)(2,1)} %param.7, s32[]{:T(128)S(6)} %min.20, s32[]{:T(128)S(6)} %min.19, s32[]{:T(128)S(6)} %min.18, ...), kind=kLoop, calls=%fused_computation.42 | loop fusion | bytes 18350100 | tf_op jit(solution)/shard_map/jit(dynamic_index_in_dim)/dynamic_slice | solution.py:57
  26.8 3.9 copy.30
  30.7 2.9 select_bitcast_fusion.3
  33.6 9.7 %collective-permute-start = (bf16[128,7168]{0,1:T(8,128)(2,1)}, bf16[128,7168]{0,1:T(8,128)(2,1)}, u32[]{:S(2)}, u32[]{:S(2)}) collective-permute-start(bf16[128,7168]{0,1:T(8,128)(2,1)} %select_bitcast_fusion.3), channel_id=1, source_target_pairs={{0,32},{16,48},{32,64},{48,80},{64,96},{80,112},{96,128},{112,144}... | collective-permute-start | bytes 5505032 | tf_op jit(solution)/shard_map/ppermute | solution.py:15
  44.0 3.9 copy.31
  47.9 41.0 %all-gather.5.cloned.1.call-done = bf16[1,512,2048]{2,1,0:T(8,128)(2,1)} async-done(((bf16[1,128,2048]{2,1,0:T(8,128)(2,1)}), bf16[1,512,2048]{2,1,0:T(8,128)(2,1)}) %all-gather.5.cloned.1.call-update) | async-done | bytes 2097168 | tf_op jit(solution)/shard_map/all_gather | solution.py:20
  88.9 0.0 all-gather.7.cloned.1.call-update
  89.0 1.4 select_bitcast_fusion.2
  90.3 12.4 %collective-permute-start.1 = (bf16[128,7168]{0,1:T(8,128)(2,1)}, bf16[128,7168]{0,1:T(8,128)(2,1)}, u32[]{:S(2)}, u32[]{:S(2)}) collective-permute-start(bf16[128,7168]{0,1:T(8,128)(2,1)} %select_bitcast_fusion.2), channel_id=1, source_target_pairs={{0,16},{16,32},{32,48},{48,64},{64,80},{80,96},{96,112},{112,128},... | collective-permute-start | bytes 5505032 | tf_op jit(solution)/shard_map/ppermute | solution.py:15
  103.3 3.9 copy.32
  107.2 2.9 select_bitcast_fusion.1
  110.1 1.9 collective-permute-start.2
  112.7 3.9 copy.33
  116.5 1.4 select_bitcast_fusion
  118.0 1.3 collective-permute-start.3
  120.6 3.9 copy.34
  124.5 0.0 collective-permute-done
  124.5 17.2 %collective-permute-done.1 = bf16[128,7168]{0,1:T(8,128)(2,1)} collective-permute-done((bf16[128,7168]{0,1:T(8,128)(2,1)}, bf16[128,7168]{0,1:T(8,128)(2,1)}, u32[]{:S(2)}, u32[]{:S(2)}) %collective-permute-start.1) | collective-permute-done | bytes 1835040 | tf_op jit(solution)/shard_map/ppermute | solution.py:15
  141.6 63.3 %collective-permute-done.2 = bf16[128,7168]{0,1:T(8,128)(2,1)} collective-permute-done((bf16[128,7168]{0,1:T(8,128)(2,1)}, bf16[128,7168]{0,1:T(8,128)(2,1)}, u32[]{:S(2)}, u32[]{:S(2)}) %collective-permute-start.2) | collective-permute-done | bytes 1835040 | tf_op jit(solution)/shard_map/ppermute | solution.py:15
  204.9 38.3 %collective-permute-done.3 = bf16[128,7168]{0,1:T(8,128)(2,1)} collective-permute-done((bf16[128,7168]{0,1:T(8,128)(2,1)}, bf16[128,7168]{0,1:T(8,128)(2,1)}, u32[]{:S(2)}, u32[]{:S(2)}) %collective-permute-start.3) | collective-permute-done | bytes 1835040 | tf_op jit(solution)/shard_map/ppermute | solution.py:15
  243.2 3.3 fusion.4
  246.5 1.6 fusion.5
  248.1 0.0 copy-start.3
  248.1 0.0 copy-start.2
  248.1 63.7 %all-to-all-start = ((bf16[128,16,448]{0,2,1:T(8,128)(2,1)}), bf16[128,16,448]{0,2,1:T(8,128)(2,1)}, u32[]{:S(2)}, u32[]{:S(2)}) async-start(bf16[128,16,448]{0,2,1:T(8,128)(2,1)} %bitcast.52), calls=%async_computation | async-start | bytes 3670016 | tf_op jit(solution)/shard_map/all_to_all | solution.py:71
  311.8 0.0 reduce-scatter.2.cloned.1.call-start
  312.5 0.0 copy-done.3
  312.5 0.6 dynamic-slice
  313.1 0.8 dynamic-update-slice
  313.8 39.9 %all-reduce = s32[4]{0:T(128)S(1)} all-reduce(s32[4]{0:T(128)S(1)} %dynamic-update-slice), channel_id=1, replica_groups=mesh['section'=16,'dp_0'=4,'dp_1'=4] {'dp_1'}, use_global_device_ids=true, to_apply=%add | all-reduce | flops 4 | bytes 32
  353.7 0.0 copy-done.2
  353.7 0.6 dynamic-slice.1
  354.9 0.2 dynamic-update-slice.1
  355.2 7.2 %all-reduce.1 = s32[16]{0:T(128)S(1)} all-reduce(s32[16]{0:T(128)S(1)} %dynamic-update-slice.1), channel_id=1, replica_groups=mesh['section'=16,'dp_0'=4,'dp_1'=4] {'dp_0'}, use_global_device_ids=true, to_apply=%add.1 | all-reduce | flops 16 | bytes 128
  362.4 0.6 reduce_sum.158
  363.7 0.1 select_reduce_fusion
  363.9 0.0 all-to-all-done
  363.9 0.0 all-gather.7.cloned.1.call-done
  363.9 0.0 copy-done
  363.9 8.6 %fusion.6 = (f32[]{:T(128)}, f32[2048,448]{0,1:T(8,128)S(1)}) fusion(f32[2048]{0:T(1024)S(1)} %get-tuple-element.13, bf16[1,2048,448]{1,2,0:T(8,128)(2,1)S(1)} %copy-done, bf16[1,2048,2048]{2,1,0:T(8,128)(2,1)} %all-gather.7.cloned.1.call-done, bf16[128,16,448]{0,2,1:T(8,128)(2,1)} %all-to-all-done), kind=kOutput, calls=%fused_computation.10 | convolution fusion | flops 3762683904 | bytes 15736836 | tf_op jit(solution)/shard_map/dot_general | solution.py:81
  372.5 0.0 copy-start.4
  372.5 1.8 copy-done.4
  374.3 6.8 %convolution_convert_fusion = bf16[2048,2048]{1,0:T(8,128)(2,1)} fusion(bf16[1,2048,448]{1,2,0:T(8,128)(2,1)S(1)} %copy-done, f32[2048,448]{0,1:T(8,128)S(1)} %get-tuple-element.23, f32[2048]{0:T(1024)S(1)} %broadcast_select_fusion), kind=kOutput, calls=%fused_computation.4 | convolution fusion | flops 3764125696 | bytes 13901824 | tf_op jit(solution)/shard_map/dot_general | solution.py:88
  381.1 0.0 reduce-scatter.2.cloned.1.call-update
  381.2 1.2 broadcast_in_dim.52
  382.4 4.3 all-to-all-start.1
  386.7 0.0 copy-start.1
  386.7 9.8 %fusion.12 = bf16[1,2048,448]{1,2,0:T(8,128)(2,1)} fusion(bf16[1,2048,2048]{2,1,0:T(8,128)(2,1)} %all-gather.7.cloned.1.call-done, f32[2048,448]{0,1:T(8,128)} %copy-done.4, f32[2048]{0:T(1024)S(1)} %broadcast_select_fusion), kind=kOutput, calls=%fused_computation.15 | convolution fusion | flops 3760848896 | bytes 13901824 | tf_op jit(solution)/shard_map/dot_general | solution.py:95
  396.5 0.0 all-to-all-done.1
  396.5 0.6 reduce_sum.173
  397.8 169.4 %reduce-scatter.2.cloned.1.call-done = bf16[128,2048]{1,0:T(8,128)(2,1)} async-done(((bf16[2048,2048]{1,0:T(8,128)(2,1)}), bf16[128,2048]{1,0:T(8,128)(2,1)}) %reduce-scatter.2.cloned.1.call-update) | async-done | bytes 524304 | tf_op jit(solution)/shard_map/reduce_scatter | solution.py:87
  567.2 0.0 copy-done.1
  (6 shorter events, 0.0 us)
Async XLA Ops:
  7.2 356.7 %copy-start = (bf16[1,2048,448]{1,2,0:T(8,128)(2,1)S(1)}, bf16[1,2048,448]{1,2,0:T(8,128)(2,1)}, u32[]{:S(2)}) copy-start(bf16[1,2048,448]{1,2,0:T(8,128)(2,1)} %param.8) | copy-start | bytes 5505028
  7.2 81.7 %all-gather.5.cloned.1.call-start = ((), (), s32[]{:S(2)}) async-start(), calls=%async_computation.4 | async-start | bytes 2621440 | tf_op jit(solution)/shard_map/all_gather | solution.py:20
  7.9 356.0 %all-gather.7.cloned.1.call-start = ((), (), s32[]{:S(2)}) async-start(), calls=%async_computation.5 | async-start | bytes 10485760 | tf_op jit(solution)/shard_map/all_gather | solution.py:20
  33.6 90.9 %collective-permute-start = (bf16[128,7168]{0,1:T(8,128)(2,1)}, bf16[128,7168]{0,1:T(8,128)(2,1)}, u32[]{:S(2)}, u32[]{:S(2)}) collective-permute-start(bf16[128,7168]{0,1:T(8,128)(2,1)} %select_bitcast_fusion.3), channel_id=1, source_target_pairs={{0,32},{16,48},{32,64},{48,80},{64,96},{80,112},{96,128},{112,144}... | collective-permute-start | bytes 5505032 | tf_op jit(solution)/shard_map/ppermute | solution.py:15
  90.3 51.3 %collective-permute-start.1 = (bf16[128,7168]{0,1:T(8,128)(2,1)}, bf16[128,7168]{0,1:T(8,128)(2,1)}, u32[]{:S(2)}, u32[]{:S(2)}) collective-permute-start(bf16[128,7168]{0,1:T(8,128)(2,1)} %select_bitcast_fusion.2), channel_id=1, source_target_pairs={{0,16},{16,32},{32,48},{48,64},{64,80},{80,96},{96,112},{112,128},... | collective-permute-start | bytes 5505032 | tf_op jit(solution)/shard_map/ppermute | solution.py:15
  110.1 94.8 %collective-permute-start.2 = (bf16[128,7168]{0,1:T(8,128)(2,1)}, bf16[128,7168]{0,1:T(8,128)(2,1)}, u32[]{:S(2)}, u32[]{:S(2)}) collective-permute-start(bf16[128,7168]{0,1:T(8,128)(2,1)} %select_bitcast_fusion.1), channel_id=1, source_target_pairs={{16,0},{32,16},{48,32},{64,48},{80,64},{96,80},{112,96},{128,112},... | collective-permute-start | bytes 5505032 | tf_op jit(solution)/shard_map/ppermute | solution.py:15
  118.0 125.2 %collective-permute-start.3 = (bf16[128,7168]{0,1:T(8,128)(2,1)}, bf16[128,7168]{0,1:T(8,128)(2,1)}, u32[]{:S(2)}, u32[]{:S(2)}) collective-permute-start(bf16[128,7168]{0,1:T(8,128)(2,1)} %select_bitcast_fusion), channel_id=1, source_target_pairs={{32,0},{48,16},{64,32},{80,48},{96,64},{112,80},{128,96},{144,112}... | collective-permute-start | bytes 5505032 | tf_op jit(solution)/shard_map/ppermute | solution.py:15
  248.1 64.4 %copy-start.3 = (u32[256]{0:T(256)S(1)}, u32[256]{0:T(256)}, u32[]{:S(2)}) copy-start(u32[256]{0:T(256)} %constant.84) | copy-start | bytes 3076
  248.1 105.6 %copy-start.2 = (u32[256]{0:T(256)S(1)}, u32[256]{0:T(256)}, u32[]{:S(2)}) copy-start(u32[256]{0:T(256)} %constant.89) | copy-start | bytes 3076
  248.1 115.8 %all-to-all-start = ((bf16[128,16,448]{0,2,1:T(8,128)(2,1)}), bf16[128,16,448]{0,2,1:T(8,128)(2,1)}, u32[]{:S(2)}, u32[]{:S(2)}) async-start(bf16[128,16,448]{0,2,1:T(8,128)(2,1)} %bitcast.52), calls=%async_computation | async-start | bytes 3670016 | tf_op jit(solution)/shard_map/all_to_all | solution.py:71
  311.8 255.5 %reduce-scatter.2.cloned.1.call-start = ((), (), s32[]{:S(2)}) async-start(), calls=%async_computation.3 | async-start | bytes 8912896 | tf_op jit(solution)/shard_map/reduce_scatter | solution.py:87
  372.5 1.8 copy-start.4
  382.4 14.1 %all-to-all-start.1 = ((f32[16,1,1]{2,1,0:T(1,128)}), f32[16,1,1]{2,1,0:T(1,128)S(1)}, u32[]{:S(2)}, u32[]{:S(2)}) async-start(f32[16,1,1]{2,1,0:T(1,128)} %broadcast_in_dim.52), calls=%async_computation.2 | async-start | bytes 16384 | tf_op jit(solution)/shard_map/all_to_all | solution.py:26
  386.7 180.5 %copy-start.1 = (bf16[1,2048,448]{1,2,0:T(8,128)(2,1)S(1)}, bf16[1,2048,448]{1,2,0:T(8,128)(2,1)}, u32[]{:S(2)}) copy-start(bf16[1,2048,448]{1,2,0:T(8,128)(2,1)} %param.8) | copy-start | bytes 5505028
Sparse Core Ops, SparseCore 0:
  9.8 79.0 all-gather.4
  90.7 227.4 all-gather.6
  381.3 185.9 reduce-scatter.1
where the time goes:
time: 576 us; the launch traced here: 575 us
  waiting for transfers between devices  330 us (57%)
  starting transfers between devices  93.4 us (16%)
  blocking collectives  47.1 us (8%)
  local copies, waits for them, and re-layouts  32.8 us (6%)
  between operations  27.9 us (5%)
  matrix products  25.2 us (4%)
  other arithmetic  18.5 us (3%)
    reduce_scatter x1, waiting for transfers between devices, per_device(): lax.psum_scatter(lax.dot_general(scaled, weights, (((1,), (1,)), ((), ())...  169 us
    ppermute x4, waiting for transfers between devices, from_behind(): return lax.ppermute(block, axis, route)  119 us
    all_to_all x1, starting transfers between devices, per_device(): lax.all_to_all(target, DP, split_axis=1, concat_axis=0, tiled=True)  63.7 us
    unnamed x2, blocking collectives  47.1 us
    all_gather x2, waiting for transfers between devices, whole_of(): x = lax.all_gather(x, axis, axis=dim, tiled=True)  41 us
    ppermute x4, starting transfers between devices, from_behind(): return lax.ppermute(block, axis, route)  25.3 us
    unnamed x21, local copies, waits for them, and re-layouts  23.5 us
  transfers between devices with their start and end apart: 9, of which 5 were waited for; matrix products, arithmetic and copies ran while one was open for 10% of the time, Pallas kernels for 0%

commit v1 on v0

--- a/solution.py
+++ b/solution.py
@@ -3,6 +3,7 @@
 from jax import lax
 from jax.sharding import Mesh
 from jax.sharding import PartitionSpec as P
+from jax.lax import all_to_all, axis_size
 
 DP = ("dp_0", "dp_1")
 loss_scale = 128.0
@@ -68,7 +69,9 @@
     target = (wide * lax.rsqrt(jnp.mean(wide * wide, axis=1, keepdims=True) + norm_eps)).astype(
         jnp.bfloat16
     )
-    columns = lax.all_to_all(target, DP, split_axis=1, concat_axis=0, tiled=True)
+    columns = jnp.concatenate(
+        all_to_all(jnp.stack(jnp.split(target, axis_size(DP), axis=1)), DP, 0, 0), axis=0
+    )
     students, counts = (whole_of(student_states[0], DP, 0), whole_of(valid_counts, DP, 0))
     per_batch = student_states.shape[1]
     token_rows = jnp.arange(students.shape[0], dtype=jnp.int32)

time: 576 us -> 586 us (1.017)
  local copies, waits for them, and re-layouts: 32.8 us -> 43.4 us
  waiting for transfers between devices: 330 us -> 340 us
  starting transfers between devices: 93.4 us -> 84.3 us
    ppermute x4, waiting for transfers between devices: 119 us -> 146 us  [from_behind(): return lax.ppermute(block, axis, route)]
    all_gather x2, waiting for transfers between devices: 41 us -> 22.9 us  [whole_of(): x = lax.all_gather(x, axis, axis=dim, tiled=True)]
    unnamed x21 -> x36, local copies, waits for them, and re-layouts: 23.5 us -> 33.3 us
    ppermute x4, starting transfers between devices: 25.3 us -> 16.1 us  [from_behind(): return lax.ppermute(block, axis, route)]
  transfers between devices with their start and end apart: 9 -> 9, of which waited for: 5 -> 6; matrix products, arithmetic and copies ran while one was open for 10% -> 12% of each run, Pallas kernels for 0% -> 0%
where the time goes in v1:
time: 586 us; the launch traced here: 585 us
  waiting for transfers between devices  340 us (58%)
  starting transfers between devices  84.3 us (14%)
  blocking collectives  47.1 us (8%)
  local copies, waits for them, and re-layouts  43.4 us (7%)
  between operations  27.8 us (5%)
  matrix products  25.2 us (4%)
  other arithmetic  17.2 us (3%)
    reduce_scatter x1, waiting for transfers between devices, per_device(): lax.psum_scatter(lax.dot_general(scaled, weights, (((1,), (1,)), ((), ())...  170 us
    ppermute x4, waiting for transfers between devices, from_behind(): return lax.ppermute(block, axis, route)  146 us
    all_to_all x1, starting transfers between devices, per_device(): all_to_all(jnp.stack(jnp.split(target, axis_size(DP), axis=1)), DP, 0, 0)  63.8 us
    unnamed x2, blocking collectives  47.1 us
    unnamed x36, local copies, waits for them, and re-layouts  33.3 us
    all_gather x2, waiting for transfers between devices, whole_of(): x = lax.all_gather(x, axis, axis=dim, tiled=True)  22.9 us
    ppermute x4, starting transfers between devices, from_behind(): return lax.ppermute(block, axis, route)  16.1 us
  transfers between devices with their start and end apart: 9, of which 6 were waited for; matrix products, arithmetic and copies ran while one was open for 12% of the time, Pallas kernels for 0%

profile of v1, /device:TPU:1, one launch (start us, length us, event | category | flops | bytes accessed | tf_op | source)
XLA Modules:
  0.0 584.9 jit_solution(14665417726846585409)
XLA Ops:
  7.2 0.0 all-gather.5.cloned.1.call-start
  7.2 0.7 all-gather.5.cloned.1.call-update
  7.9 0.0 all-gather.7.cloned.1.call-start
  8.0 0.7 slice.3
  8.7 1.3 fusion.52
  10.0 0.8 convert_reduce_fusion
  10.9 1.5 fusion.42
  19.2 7.5 %constant_dynamic-slice_fusion = (bf16[1,128,7168]{2,1,0:T(8,128)(2,1)}, bf16[1,128,7168]{2,1,0:T(8,128)(2,1)}, bf16[1,128,7168]{2,1,0:T(8,128)(2,1)}, bf16[1,128,7168]{2,1,0:T(8,128)(2,1)}, bf16[1,128,7168]{2,1,0:T(8,128)(2,1)}) fusion(bf16[4,128,7168]{2,1,0:T(8,128)(2,1)} %param.7, s32[]{:T(128)S(6)} %min.20, s32[]{:T(128)S(6)} %min.19, s32[]{:T(128)S(6)} %min.18, ...), kind=kLoop, calls=%fused_computation.74 | loop fusion | bytes 18350100 | tf_op jit(solution)/shard_map/jit(dynamic_index_in_dim)/dynamic_slice | solution.py:58
  26.7 3.9 copy.30
  30.6 2.9 select_bitcast_fusion.3
  33.5 9.7 %collective-permute-start = (bf16[128,7168]{0,1:T(8,128)(2,1)}, bf16[128,7168]{0,1:T(8,128)(2,1)}, u32[]{:S(2)}, u32[]{:S(2)}) collective-permute-start(bf16[128,7168]{0,1:T(8,128)(2,1)} %select_bitcast_fusion.3), channel_id=1, source_target_pairs={{0,32},{16,48},{32,64},{48,80},{64,96},{80,112},{96,128},{112,144}... | collective-permute-start | bytes 5505032 | tf_op jit(solution)/shard_map/ppermute | solution.py:16
  43.8 3.9 copy.31
  47.7 1.4 select_bitcast_fusion.2
  49.1 2.4 collective-permute-start.1
  52.2 3.9 copy.32
  56.1 2.9 select_bitcast_fusion.1
  59.0 2.7 collective-permute-start.2
  62.4 3.9 copy.33
  66.3 22.8 %all-gather.5.cloned.1.call-done = bf16[1,512,2048]{2,1,0:T(8,128)(2,1)} async-done(((bf16[1,128,2048]{2,1,0:T(8,128)(2,1)}), bf16[1,512,2048]{2,1,0:T(8,128)(2,1)}) %all-gather.5.cloned.1.call-update) | async-done | bytes 2097168 | tf_op jit(solution)/shard_map/all_gather | solution.py:21
  89.1 0.0 all-gather.7.cloned.1.call-update
  89.1 1.4 select_bitcast_fusion
  90.5 1.3 collective-permute-start.3
  93.1 3.9 copy.34
  97.0 17.4 %collective-permute-done = bf16[128,7168]{0,1:T(8,128)(2,1)} collective-permute-done((bf16[128,7168]{0,1:T(8,128)(2,1)}, bf16[128,7168]{0,1:T(8,128)(2,1)}, u32[]{:S(2)}, u32[]{:S(2)}) %collective-permute-start) | collective-permute-done | bytes 1835040 | tf_op jit(solution)/shard_map/ppermute | solution.py:16
  114.3 27.4 %collective-permute-done.1 = bf16[128,7168]{0,1:T(8,128)(2,1)} collective-permute-done((bf16[128,7168]{0,1:T(8,128)(2,1)}, bf16[128,7168]{0,1:T(8,128)(2,1)}, u32[]{:S(2)}, u32[]{:S(2)}) %collective-permute-start.1) | collective-permute-done | bytes 1835040 | tf_op jit(solution)/shard_map/ppermute | solution.py:16
  141.7 63.2 %collective-permute-done.2 = bf16[128,7168]{0,1:T(8,128)(2,1)} collective-permute-done((bf16[128,7168]{0,1:T(8,128)(2,1)}, bf16[128,7168]{0,1:T(8,128)(2,1)}, u32[]{:S(2)}, u32[]{:S(2)}) %collective-permute-start.2) | collective-permute-done | bytes 1835040 | tf_op jit(solution)/shard_map/ppermute | solution.py:16
  204.9 38.3 %collective-permute-done.3 = bf16[128,7168]{0,1:T(8,128)(2,1)} collective-permute-done((bf16[128,7168]{0,1:T(8,128)(2,1)}, bf16[128,7168]{0,1:T(8,128)(2,1)}, u32[]{:S(2)}, u32[]{:S(2)}) %collective-permute-start.3) | collective-permute-done | bytes 1835040 | tf_op jit(solution)/shard_map/ppermute | solution.py:16
  243.2 3.3 fusion.4
  246.5 0.4 fusion.5
  246.8 0.7 fusion.35
  247.5 0.7 fusion.34
  248.2 0.7 fusion.33
  248.8 0.7 fusion.32
  249.5 0.7 fusion.31
  250.1 0.7 fusion.30
  250.8 0.7 fusion.29
  251.4 0.7 fusion.28
  252.1 0.7 fusion.27
  252.7 0.7 fusion.26
  253.4 0.7 fusion.25
  254.0 0.7 fusion.24
  254.7 0.7 fusion.23
  255.3 0.7 fusion.22
  256.0 0.7 fusion.21
  256.7 0.7 fusion.20
  257.3 63.8 %all-to-all-start = ((bf16[16,128,448]{1,2,0:T(8,128)(2,1)}), bf16[16,128,448]{1,2,0:T(8,128)(2,1)}, u32[]{:S(2)}, u32[]{:S(2)}) async-start(bf16[16,128,448]{1,2,0:T(8,128)(2,1)} %fusion.20), calls=%async_computation | async-start | bytes 3670016 | tf_op jit(solution)/shard_map/all_to_all | solution.py:73
  321.1 0.0 reduce-scatter.2.cloned.1.call-start
  321.8 0.6 dynamic-slice
  322.4 0.8 dynamic-update-slice
  323.2 39.9 %all-reduce = s32[4]{0:T(128)S(1)} all-reduce(s32[4]{0:T(128)S(1)} %dynamic-update-slice), channel_id=1, replica_groups=mesh['section'=16,'dp_0'=4,'dp_1'=4] {'dp_1'}, use_global_device_ids=true, to_apply=%add | all-reduce | flops 4 | bytes 32
  363.1 0.6 dynamic-slice.1
  364.3 0.2 dynamic-update-slice.1
  364.5 7.2 %all-reduce.1 = s32[16]{0:T(128)S(1)} all-reduce(s32[16]{0:T(128)S(1)} %dynamic-update-slice.1), channel_id=1, replica_groups=mesh['section'=16,'dp_0'=4,'dp_1'=4] {'dp_0'}, use_global_device_ids=true, to_apply=%add.1 | all-reduce | flops 16 | bytes 128
  371.7 0.6 reduce_sum.158
  373.1 0.1 select_reduce_fusion
  373.2 0.0 all-gather.7.cloned.1.call-done
  373.3 8.6 %fusion.6 = (f32[]{:T(128)}, f32[2048,448]{0,1:T(8,128)S(1)}) fusion(f32[2048]{0:T(1024)S(1)} %get-tuple-element.13, bf16[1,2048,448]{1,2,0:T(8,128)(2,1)S(1)} %copy-done, bf16[1,2048,2048]{2,1,0:T(8,128)(2,1)} %all-gather.7.cloned.1.call-done, bf16[16,128,448]{1,2,0:T(8,128)(2,1)} %all-to-all-done), kind=kOutput, calls=%fused_computation.10 | convolution fusion | flops 3762683904 | bytes 15736836 | tf_op jit(solution)/shard_map/dot_general | solution.py:84
  381.9 1.8 copy-done.4
  383.7 6.8 %convolution_convert_fusion = bf16[2048,2048]{1,0:T(8,128)(2,1)} fusion(bf16[1,2048,448]{1,2,0:T(8,128)(2,1)S(1)} %copy-done, f32[2048,448]{0,1:T(8,128)S(1)} %get-tuple-element.23, f32[2048]{0:T(1024)S(1)} %broadcast_select_fusion), kind=kOutput, calls=%fused_computation.4 | convolution fusion | flops 3764125696 | bytes 13901824 | tf_op jit(solution)/shard_map/dot_general | solution.py:91
  390.5 1.2 broadcast_in_dim.52
  391.8 4.3 all-to-all-start.1
  396.1 9.8 %fusion.12 = bf16[1,2048,448]{1,2,0:T(8,128)(2,1)} fusion(bf16[1,2048,2048]{2,1,0:T(8,128)(2,1)} %all-gather.7.cloned.1.call-done, f32[2048,448]{0,1:T(8,128)} %copy-done.4, f32[2048]{0:T(1024)S(1)} %broadcast_select_fusion), kind=kOutput, calls=%fused_computation.15 | convolution fusion | flops 3760848896 | bytes 13901824 | tf_op jit(solution)/shard_map/dot_general | solution.py:98
  405.9 0.6 reduce_sum.173
  407.2 170.1 %reduce-scatter.2.cloned.1.call-done = bf16[128,2048]{1,0:T(8,128)(2,1)} async-done(((bf16[2048,2048]{1,0:T(8,128)(2,1)}), bf16[128,2048]{1,0:T(8,128)(2,1)}) %reduce-scatter.2.cloned.1.call-update) | async-done | bytes 524304 | tf_op jit(solution)/shard_map/reduce_scatter | solution.py:90
  (18 shorter events, 0.1 us)
Async XLA Ops:
  7.2 366.1 %copy-start = (bf16[1,2048,448]{1,2,0:T(8,128)(2,1)S(1)}, bf16[1,2048,448]{1,2,0:T(8,128)(2,1)}, u32[]{:S(2)}) copy-start(bf16[1,2048,448]{1,2,0:T(8,128)(2,1)} %param.8) | copy-start | bytes 5505028
  7.2 81.9 %all-gather.5.cloned.1.call-start = ((), (), s32[]{:S(2)}) async-start(), calls=%async_computation.4 | async-start | bytes 2621440 | tf_op jit(solution)/shard_map/all_gather | solution.py:21
  7.9 365.3 %all-gather.7.cloned.1.call-start = ((), (), s32[]{:S(2)}) async-start(), calls=%async_computation.5 | async-start | bytes 10485760 | tf_op jit(solution)/shard_map/all_gather | solution.py:21
  33.5 80.8 %collective-permute-start = (bf16[128,7168]{0,1:T(8,128)(2,1)}, bf16[128,7168]{0,1:T(8,128)(2,1)}, u32[]{:S(2)}, u32[]{:S(2)}) collective-permute-start(bf16[128,7168]{0,1:T(8,128)(2,1)} %select_bitcast_fusion.3), channel_id=1, source_target_pairs={{0,32},{16,48},{32,64},{48,80},{64,96},{80,112},{96,128},{112,144}... | collective-permute-start | bytes 5505032 | tf_op jit(solution)/shard_map/ppermute | solution.py:16
  49.1 92.6 %collective-permute-start.1 = (bf16[128,7168]{0,1:T(8,128)(2,1)}, bf16[128,7168]{0,1:T(8,128)(2,1)}, u32[]{:S(2)}, u32[]{:S(2)}) collective-permute-start(bf16[128,7168]{0,1:T(8,128)(2,1)} %select_bitcast_fusion.2), channel_id=1, source_target_pairs={{0,16},{16,32},{32,48},{48,64},{64,80},{80,96},{96,112},{112,128},... | collective-permute-start | bytes 5505032 | tf_op jit(solution)/shard_map/ppermute | solution.py:16
  59.0 145.9 %collective-permute-start.2 = (bf16[128,7168]{0,1:T(8,128)(2,1)}, bf16[128,7168]{0,1:T(8,128)(2,1)}, u32[]{:S(2)}, u32[]{:S(2)}) collective-permute-start(bf16[128,7168]{0,1:T(8,128)(2,1)} %select_bitcast_fusion.1), channel_id=1, source_target_pairs={{16,0},{32,16},{48,32},{64,48},{80,64},{96,80},{112,96},{128,112},... | collective-permute-start | bytes 5505032 | tf_op jit(solution)/shard_map/ppermute | solution.py:16
  90.5 152.7 %collective-permute-start.3 = (bf16[128,7168]{0,1:T(8,128)(2,1)}, bf16[128,7168]{0,1:T(8,128)(2,1)}, u32[]{:S(2)}, u32[]{:S(2)}) collective-permute-start(bf16[128,7168]{0,1:T(8,128)(2,1)} %select_bitcast_fusion), channel_id=1, source_target_pairs={{32,0},{48,16},{64,32},{80,48},{96,64},{112,80},{128,96},{144,112}... | collective-permute-start | bytes 5505032 | tf_op jit(solution)/shard_map/ppermute | solution.py:16
  257.3 64.5 %copy-start.3 = (u32[256]{0:T(256)S(1)}, u32[256]{0:T(256)}, u32[]{:S(2)}) copy-start(u32[256]{0:T(256)} %constant.84) | copy-start | bytes 3076
  257.3 105.7 %copy-start.2 = (u32[256]{0:T(256)S(1)}, u32[256]{0:T(256)}, u32[]{:S(2)}) copy-start(u32[256]{0:T(256)} %constant.89) | copy-start | bytes 3076
  257.3 115.9 %all-to-all-start = ((bf16[16,128,448]{1,2,0:T(8,128)(2,1)}), bf16[16,128,448]{1,2,0:T(8,128)(2,1)}, u32[]{:S(2)}, u32[]{:S(2)}) async-start(bf16[16,128,448]{1,2,0:T(8,128)(2,1)} %fusion.20), calls=%async_computation | async-start | bytes 3670016 | tf_op jit(solution)/shard_map/all_to_all | solution.py:73
  321.1 256.2 %reduce-scatter.2.cloned.1.call-start = ((), (), s32[]{:S(2)}) async-start(), calls=%async_computation.3 | async-start | bytes 8912896 | tf_op jit(solution)/shard_map/reduce_scatter | solution.py:90
  381.9 1.8 copy-start.4
  391.8 14.1 %all-to-all-start.1 = ((f32[16,1,1]{2,1,0:T(1,128)}), f32[16,1,1]{2,1,0:T(1,128)S(1)}, u32[]{:S(2)}, u32[]{:S(2)}) async-start(f32[16,1,1]{2,1,0:T(1,128)} %broadcast_in_dim.52), calls=%async_computation.2 | async-start | bytes 16384 | tf_op jit(solution)/shard_map/all_to_all | solution.py:27
  396.1 181.2 %copy-start.1 = (bf16[1,2048,448]{1,2,0:T(8,128)(2,1)S(1)}, bf16[1,2048,448]{1,2,0:T(8,128)(2,1)}, u32[]{:S(2)}) copy-start(bf16[1,2048,448]{1,2,0:T(8,128)(2,1)} %param.8) | copy-start | bytes 5505028
Sparse Core Ops, SparseCore 0:
  9.8 79.2 all-gather.4
  90.9 225.9 all-gather.6
  390.6 186.6 reduce-scatter.1
